TPU v7x, 32 devices: a whole 2x2x4 slice. The times are simulated.
32 devices in a mesh: dp: 16 (over z, y, core), tensor: 2 (over x).
Axes of the slice: x: 2, y: 2, z: 4, core: 2. Of those that a mesh axis runs over, the one named last changes fastest.
Arguments:
- expert_act: bfloat16 [16384, 2880], P(('dp', 'tensor')), may hold values from -6 to 6
- grad_out: bfloat16 [32768, 1440], P(('dp', 'tensor')), may hold values from -6 to 6
- slot_token: int32 [16384], P(('dp', 'tensor')), may hold values from 0 to 1023, as said below
- slot_prob: float32 [16384], P(('dp', 'tensor')), may hold values from 0.2 to 1
- live_count: int32 [32], P(('dp', 'tensor')), may hold values from 128 to 512, as said below
Outputs:
- weight_grad: float32 [2880, 1440], P('dp', 'tensor')
Inputs may be any that keep to these rules, and one draw needn't show every extreme that they name: `slot_token`: each device's 512 entries are distinct token indices of that device. `live_count`: each entry is 512 // j for some j of 1 to 4.
All inputs are finite; a program needn't handle non-finite values.
Results may differ from a plain program's by a relative error of at most 0.0029.
Values may be sent and summed in bfloat16 or wider, within the bound.
No kernel may reach another device: no remote copies, remote signals or barrier semaphores. Data moves between devices by JAX's collectives and lax.ppermute only.
A program may use at most 128 MiB of HBM per device.

v0:
```python
import math
import jax
import jax.numpy as jnp
from jax import lax
from jax.sharding import PartitionSpec as P


def contract(left, right):
    return lax.dot_general(
        left, right, (((0,), (0,)), ((), ())), preferred_element_type=jnp.float32
    )


def shards(expert_act, grad_out, slot_token, slot_prob, live_count):
    slot_count = expert_act.shape[0]
    devices = lax.axis_size("dp") * lax.axis_size("tensor")
    scaling = 1.0 / math.sqrt(slot_count * devices)
    position = jnp.arange(slot_count, dtype=jnp.int32)
    live_mask = position < live_count[0]
    weighting = jnp.where(live_mask, slot_prob, jnp.zeros_like(slot_prob))
    picked = jnp.take(grad_out, slot_token, axis=0).astype(jnp.float32)
    weighted = (picked * weighting[:, None]).astype(jnp.bfloat16)
    both_acts = lax.all_gather(expert_act, "tensor", axis=0, tiled=True)
    both_grads = lax.all_to_all(weighted, "tensor", split_axis=1, concat_axis=0, tiled=True)
    gradient = lax.psum_scatter(
        contract(both_acts, both_grads), "dp", scatter_dimension=0, tiled=True
    )
    return gradient * scaling


def solution(mesh):
    return jax.shard_map(
        shards,
        mesh=mesh,
        in_specs=(
            P(("dp", "tensor"), None),
            P(("dp", "tensor"), None),
            P(("dp", "tensor")),
            P(("dp", "tensor")),
            P(("dp", "tensor")),
        ),
        out_specs=P("dp", "tensor"),
        check_vma=False,
    )
```

profile of v0, /device:TPU:0, one launch (start us, length us, event | category | flops | bytes accessed | tf_op | source)
XLA Modules:
  0.0 293.3 jit_solution(11381292390871192183)
XLA Ops:
  6.5 0.0 all-gather.2.cloned.1.call-start
  6.5 0.7 all-gather.2.cloned.1.call-update
  7.3 0.0 copy-start
  7.3 0.0 all-reduce.3.cloned.1.call-start
  7.3 3.1 %copy.16 = bf16[1024,1440]{1,0:T(8,128)(2,1)S(1)} copy(bf16[1024,1440]{0,1:T(8,128)(2,1)} %param.6) | data formatting | bytes 5898240 | tf_op args[1]
  10.5 0.0 copy-done
  10.5 3.0 %gather_fusion = bf16[512,1440]{1,0:T(8,128)(2,1)} fusion(bf16[1024,1440]{1,0:T(8,128)(2,1)S(1)} %copy.16, s32[1024]{0:T(1024)S(1)} %pad_clamp_fusion), kind=kCustom, calls=%fused_computation | custom fusion | bytes 2951168 | tf_op jit(solution)/shard_map/jit(_take)/gather | solution.py:21
  13.5 0.0 copy-start.1
  13.5 1.7 copy.17
  15.8 0.0 copy-done.1
  15.9 0.4 multiply_convert_fusion
  16.3 37.9 %all_to_all.16 = bf16[512,2,720]{0,2,1:T(8,128)(2,1)S(1)} all-to-all(bf16[512,2,720]{0,2,1:T(8,128)(2,1)S(1)} %multiply_convert_fusion), channel_id=1, replica_groups=mesh['dp'=16,'tensor'=2] {'tensor'}, dimensions={1} | all-to-all | bytes 2949120 | tf_op jit(solution)/shard_map/all_to_all | solution.py:24
  54.1 0.2 copy.22
  54.3 47.6 %all-gather.2.cloned.1.call-done = bf16[1024,2880]{0,1:T(8,128)(2,1)} async-done(((bf16[512,2880]{0,1:T(8,128)(2,1)}), bf16[1024,2880]{0,1:T(8,128)(2,1)}) %all-gather.2.cloned.1.call-update) | async-done | bytes 5898256 | tf_op jit(solution)/shard_map/all_gather | solution.py:23
  101.9 9.6 %convolution_bitcast_fusion = f32[2880,720]{0,1:T(8,128)} fusion(bf16[1024,720]{0,1:T(8,128)(2,1)S(1)} %bitcast.15, bf16[1024,2880]{0,1:T(8,128)(2,1)} %all-gather.2.cloned.1.call-done), kind=kOutput, calls=%fused_computation.1 | convolution fusion | flops 4246732800 | bytes 15667200 | tf_op jit(solution)/shard_map/dot_general | solution.py:9
  111.5 0.0 copy-start.2
  111.5 0.0 all-reduce.3.cloned.1.call-update
  111.6 0.6 copy-done.2
  112.2 0.6 dynamic-slice
  113.4 170.4 %all-reduce.3.cloned.1.call-done = f32[2880,720]{0,1:T(8,128)} async-done(((f32[2880,720]{0,1:T(8,128)}), f32[2880,720]{0,1:T(8,128)}) %all-reduce.3.cloned.1.call-update) | async-done | bytes 8294416
  283.8 1.5 constant_dynamic-slice_fusion
  285.3 0.2 copy.19
  285.6 0.8 broadcast_multiply_fusion
  (4 shorter events, 0.0 us)
Async XLA Ops:
  6.5 95.4 %all-gather.2.cloned.1.call-start = ((), (), s32[]{:S(2)}) async-start(), calls=%async_computation.1 | async-start | bytes 8847360 | tf_op jit(solution)/shard_map/all_gather | solution.py:23
  7.3 3.2 %copy-start = (s32[512]{0:T(512)S(1)}, s32[512]{0:T(512)}, u32[]{:S(2)}) copy-start(s32[512]{0:T(512)} %param.7) | copy-start | bytes 6148
  7.3 276.6 %all-reduce.3.cloned.1.call-start = ((), (), s32[]{:S(2)}) async-start(), calls=%async_computation.2 | async-start | bytes 16957440
  13.5 2.4 copy-start.1
  111.5 0.7 copy-start.2
Sparse Core Ops, SparseCore 0:
  8.9 92.9 all-gather.1
  111.7 172.0 all-reduce.2
where the time goes:
time: 294 us; the launch traced here: 293 us
  waiting for transfers between devices  219 us (74%)
  blocking collectives  37.9 us (13%)
  between operations  14.8 us (5%)
  local copies, waits for them, and re-layouts  10.9 us (4%)
  matrix products  9.64 us (3%)
    unnamed x3, waiting for transfers between devices  171 us
    all_gather x1, waiting for transfers between devices, shards(): both_acts = lax.all_gather(expert_act, 'tensor', axis=0, tiled=True)  47.6 us
    all_to_all x1, blocking collectives, shards(): lax.all_to_all(weighted, 'tensor', split_axis=1, concat_axis=0, tiled=True)  37.9 us
    dot_general x1, matrix products, contract(): lax.dot_general(left, right, (((0,), (0,)), ((), ())), preferred_element_...  9.64 us
  transfers between devices with their start and end apart: 2, of which 2 were waited for; matrix products, arithmetic and copies ran while one was open for 3% of the time, Pallas kernels for 0%

commit v1 on v0

--- a/solution.py
+++ b/solution.py
@@ -21,7 +21,12 @@
     picked = jnp.take(grad_out, slot_token, axis=0).astype(jnp.float32)
     weighted = (picked * weighting[:, None]).astype(jnp.bfloat16)
     both_acts = lax.all_gather(expert_act, "tensor", axis=0, tiled=True)
-    both_grads = lax.all_to_all(weighted, "tensor", split_axis=1, concat_axis=0, tiled=True)
+    both_grads = jnp.concatenate(
+        lax.all_to_all(
+            jnp.stack(jnp.split(weighted, lax.axis_size("tensor"), axis=1)), "tensor", 0, 0
+        ),
+        axis=0,
+    )
     gradient = lax.psum_scatter(
         contract(both_acts, both_grads), "dp", scatter_dimension=0, tiled=True
     )

time: 294 us -> 295 us (level)
  no operation moved by 1% of the time
where the time goes in v1:
time: 295 us; the launch traced here: 294 us
  waiting for transfers between devices  218 us (74%)
  blocking collectives  38.5 us (13%)
  between operations  14.8 us (5%)
  local copies, waits for them, and re-layouts  10.4 us (4%)
  matrix products  9.65 us (3%)
    unnamed x3, waiting for transfers between devices  171 us
    all_gather x1, waiting for transfers between devices, shards(): both_acts = lax.all_gather(expert_act, 'tensor', axis=0, tiled=True)  47 us
    all_to_all x1, blocking collectives, shards(): lax.all_to_all(jnp.stack(jnp.split(weighted, lax.axis_size('tensor'), axi...  38.5 us
    dot_general x1, matrix products, contract(): lax.dot_general(left, right, (((0,), (0,)), ((), ())), preferred_element_...  9.65 us
  transfers between devices with their start and end apart: 2, of which 2 were waited for; matrix products, arithmetic and copies ran while one was open for 3% of the time, Pallas kernels for 0%

profile of v1, /device:TPU:0, one launch (start us, length us, event | category | flops | bytes accessed | tf_op | source)
XLA Modules:
  0.0 294.2 jit_solution(1808262338059684149)
XLA Ops:
  6.5 0.0 all-gather.2.cloned.1.call-start
  6.5 0.7 all-gather.2.cloned.1.call-update
  7.3 0.0 copy-start
  7.3 0.0 all-reduce.3.cloned.1.call-start
  7.3 3.1 %copy.15 = bf16[1024,1440]{1,0:T(8,128)(2,1)S(1)} copy(bf16[1024,1440]{0,1:T(8,128)(2,1)} %param.6) | data formatting | bytes 5898240 | tf_op args[1]
  11.1 0.0 copy-done
  11.1 0.0 copy-start.1
  11.2 3.0 %gather_fusion = bf16[512,1440]{1,0:T(8,128)(2,1)} fusion(bf16[1024,1440]{1,0:T(8,128)(2,1)S(1)} %copy.15, s32[1024]{0:T(1024)S(1)} %pad_clamp_fusion), kind=kCustom, calls=%fused_computation | custom fusion | bytes 2951168 | tf_op jit(solution)/shard_map/jit(_take)/gather | solution.py:21
  14.1 0.0 copy-done.1
  14.2 1.8 multiply_convert_fusion
  16.0 0.5 slice_bitcast_fusion.1
  16.5 0.2 pad_maximum_fusion
  16.6 0.7 copy.16
  17.3 38.5 %all_to_all.5 = bf16[2,512,720]{1,2,0:T(8,128)(2,1)S(1)} all-to-all(bf16[2,512,720]{1,2,0:T(8,128)(2,1)S(1)} %copy.16), channel_id=1, replica_groups=mesh['dp'=16,'tensor'=2] {'tensor'}, dimensions={0} | all-to-all | bytes 2949120 | tf_op jit(solution)/shard_map/all_to_all | solution.py:25
  55.8 0.2 copy.21
  56.0 47.0 %all-gather.2.cloned.1.call-done = bf16[1024,2880]{0,1:T(8,128)(2,1)} async-done(((bf16[512,2880]{0,1:T(8,128)(2,1)}), bf16[1024,2880]{0,1:T(8,128)(2,1)}) %all-gather.2.cloned.1.call-update) | async-done | bytes 5898256 | tf_op jit(solution)/shard_map/all_gather | solution.py:23
  103.0 9.7 %convolution_bitcast_fusion = f32[2880,720]{0,1:T(8,128)} fusion(bf16[1024,720]{0,1:T(8,128)(2,1)S(1)} %bitcast.16, bf16[1024,2880]{0,1:T(8,128)(2,1)} %all-gather.2.cloned.1.call-done), kind=kOutput, calls=%fused_computation.1 | convolution fusion | flops 4246732800 | bytes 15667200 | tf_op jit(solution)/shard_map/dot_general | solution.py:9
  112.6 0.0 copy-start.2
  112.6 0.0 all-reduce.3.cloned.1.call-update
  112.6 0.6 copy-done.2
  113.3 0.6 dynamic-slice
  114.5 170.3 %all-reduce.3.cloned.1.call-done = f32[2880,720]{0,1:T(8,128)} async-done(((f32[2880,720]{0,1:T(8,128)}), f32[2880,720]{0,1:T(8,128)}) %all-reduce.3.cloned.1.call-update) | async-done | bytes 8294416
  284.8 1.5 constant_dynamic-slice_fusion
  286.3 0.2 copy.18
  286.5 0.8 broadcast_multiply_fusion
  (4 shorter events, 0.0 us)
Async XLA Ops:
  6.5 96.4 %all-gather.2.cloned.1.call-start = ((), (), s32[]{:S(2)}) async-start(), calls=%async_computation.1 | async-start | bytes 8847360 | tf_op jit(solution)/shard_map/all_gather | solution.py:23
  7.3 3.9 %copy-start = (s32[512]{0:T(512)S(1)}, s32[512]{0:T(512)}, u32[]{:S(2)}) copy-start(s32[512]{0:T(512)} %param.7) | copy-start | bytes 6148
  7.3 277.5 %all-reduce.3.cloned.1.call-start = ((), (), s32[]{:S(2)}) async-start(), calls=%async_computation.2 | async-start | bytes 16957440
  11.1 3.0 %copy-start.1 = (f32[512]{0:T(512)S(1)}, f32[512]{0:T(512)}, u32[]{:S(2)}) copy-start(f32[512]{0:T(512)} %param.8) | copy-start | bytes 6148
  112.6 0.7 copy-start.2
Sparse Core Ops, SparseCore 0:
  8.9 94.0 all-gather.1
  112.8 171.9 all-reduce.2
